TPU v7x, 32 devices: a 4x4x1 block of a 4x4x8 slice. The times are simulated.
32 devices in a mesh: layer: 1 (over z), col: 4 (over y), row: 8 (over x, core).
Axes of the slice: x: 4, y: 4, z: 1, core: 2. Of those that a mesh axis runs over, the one named last changes fastest.
The devices are a block of a 4x4x8 slice.
Arguments:
- weight: float32 [1024, 4096], P(('layer', 'row'), 'col')
- grad_in: float32 [1024, 4096], P(('layer', 'row'), 'col')
- mom_first: float32 [1024, 4096], P(('layer', 'row'), 'col')
- mom_second: float32 [1024, 4096], P(('layer', 'row'), 'col')
- stat_left: float32 [1024, 1024], P(('layer', 'row'), 'col')
- stat_right: float32 [4096, 4096], P(('layer', 'row'), 'col')
- basis_left: float32 [1024, 1024], P(('layer', 'row'), 'col')
- basis_right: float32 [4096, 4096], P(('layer', 'row'), 'col')
Outputs:
- output 1: float32 [1024, 4096], P(('layer', 'row'), 'col')
- output 2: float32 [1024, 4096], P(('layer', 'row'), 'col')
- output 3: float32 [1024, 4096], P(('layer', 'row'), 'col')
- output 4: float32 [1024, 1024], P(('layer', 'row'), 'col')
- output 5: float32 [4096, 4096], P(('layer', 'row'), 'col')
All inputs are finite; a program needn't handle non-finite values.
Results may differ from a plain program's by a relative error of at most 0.001.
Values are sent between devices in bfloat16 or wider.
A program may use at most 768 MiB of HBM per device.

v0:
```python
import functools

import jax
import jax.numpy as jnp
from jax import lax
from jax.experimental import pallas as pl
from jax.experimental.pallas import tpu as pltpu
from jax.sharding import PartitionSpec as P

BETA1 = 0.9
BETA2 = 0.9
EPS = 1e-8
LR = 0.1
STEP = 10
BIAS_ONE = 1.0 - BETA1 ** STEP
BIAS_TWO = 1.0 - BETA2 ** STEP
MESH = pl.DeviceIdType.MESH
HIGHEST = lax.Precision.HIGHEST
F32 = jnp.float32
BF16 = jnp.bfloat16
NN = (((1,), (0,)), ((), ()))
TN = (((0,), (0,)), ((), ()))
NT = (((1,), (1,)), ((), ()))
COUNTS = (7, 55, 7)


def dot(a, b, dims, precision=None):
    return lax.dot_general(a, b, dims, precision=precision, preferred_element_type=F32)


def kernel(nx, ny, w_ref, g_ref, m_ref, v_ref, l_ref, r_ref, ql_ref, qr_ref,
           ow_ref, om_ref, ov_ref, ol_ref, or_ref,
           qr_f, qr_b, qr_t, grow, growb, ql_f, ql_row, ql_send, ql_col, gx, gy, hb, nb,
           acc, gacc, up, rin, lp, lrecv, lx, wbuf, mbuf, vbuf,
           send_sem, recv_sem, local_sem):
    row = lax.axis_index("row")
    col = lax.axis_index("col")
    core = lax.rem(row, 2)
    x = lax.div(row, 2)
    nrow = 2 * nx
    rb, cb = w_ref.shape
    kb = qr_ref.shape[0]
    lb = ql_ref.shape[1]
    hr = rb // 2
    qb = rb // ny

    def wrap(v, n):
        return lax.rem(v + n, n)

    x_plus = {"row": wrap(row + 2, nrow)}
    x_minus = {"row": wrap(row - 2, nrow)}
    partner = {"row": row + 1 - 2 * core}
    y_plus = {"col": wrap(col + 1, ny)}
    y_minus = {"col": wrap(col - 1, ny)}
    prow = row + 1 - 2 * core
    counts = {"send": 0, "recv": 0, "local": 0}
    pending = []

    def new(kind):
        counts[kind] += 1
        return counts[kind] - 1

    def remote(src, dst, device, send, recv=None):
        recv = new("recv") if recv is None else recv
        return pltpu.make_async_remote_copy(
            src_ref=src, dst_ref=dst, send_sem=send_sem.at[send], recv_sem=recv_sem.at[recv],
            device_id=device, device_id_type=MESH)

    def sends(span):
        i = new("send")
        pending.append(remote(span, span, partner, i, 0))
        return i

    snd_qr, snd_rows = sends(qr_b.at[pl.ds(0, nrow - 1)]), sends(qr_b.at[pl.ds(0, nrow - 1)])
    snd_g, snd_small = sends(qr_b.at[pl.ds(0, 3)]), sends(gx.at[pl.ds(0, 5)])
    snd_ql, snd_gx = sends(ql_col.at[pl.ds(0, nrow - 1), 0]), sends(gx.at[pl.ds(0, nrow - 1), 0])
    snd_u = sends(rin)

    def arrived(span, recv):
        remote(span, span, partner, 0, recv).wait_recv()

    def local(src, dst, sem=None):
        copy = pltpu.make_async_copy(src, dst, local_sem.at[new("local") if sem is None else sem])
        copy.start()
        return copy

    class Gather8:
        def __init__(self, at, own, span, snd, cut=lambda ref: [ref], first=lambda ref: [ref], share=None):
            lft, rgt, far = wrap(row - 2, nrow), wrap(row + 2, nrow), wrap(row + 4, nrow)
            self.span = span
            self.at, self.lft, self.rgt = at, lft, rgt
            self.second_sem, self.a0_sem, self.b1_sem = (new("recv") for _ in range(3))
            self.own_sem, self.near_sem, self.far_sem = share or [new("recv") for _ in range(3)]
            self.a0 = [remote(c, d, x_plus, snd, self.a0_sem) for c, d in zip(first(own(0)), first(at(row, 0)))]
            self.b1 = [remote(c, d, x_minus, snd, self.b1_sem) for c, d in zip(first(own(1)), first(at(row, 1)))]
            self.a1 = remote(own(1), at(row, 1), x_plus, snd, self.second_sem)
            self.b0 = remote(own(0), at(row, 0), x_minus, snd, self.second_sem)
            self.p = [remote(own(h), at(row, h), partner, snd, self.own_sem) for h in (0, 1)]
            self.f_sem = [new("recv") for _ in cut(at(lft, 0))]
            self.f0 = [remote(c, c, x_plus, snd, i) for c, i in zip(cut(at(lft, 0)), self.f_sem)]
            self.f1 = [remote(c, c, x_minus, snd, i) for c, i in zip(cut(at(rgt, 1)), self.f_sem)]
            self.part = cut(at(far, 0))
            if len(self.part) > 1:
                self.two = at(far, 0).at[pl.ds(0, 2 * self.part[0].shape[0])]
            self.near = [remote(at(s, h), at(s, h), partner, snd, self.near_sem)
                         for s, h in ((lft, 0), (rgt, 1), (lft, 1), (rgt, 0))]
            self.last = [[remote(c, c, partner, snd, self.far_sem) for c in cut(at(far, h))] for h in (0, 1)]

        def early(self):
            for c in (*self.a0, *self.b1):
                c.start()

        def later(self):
            self.a1.start()
            self.b0.start()

        def to_partner(self):
            for c in self.p:
                c.start()

        def start(self):
            self.early()
            self.later()
            self.to_partner()

        def forward(self):
            arrived(self.at(self.lft, 0), self.a0_sem)
            for c in self.f0:
                c.start()
            self.near[0].start()
            arrived(self.at(self.rgt, 1), self.b1_sem)
            for c in self.f1:
                c.start()
            self.near[1].start()

        def second(self):
            arrived(self.span(1), self.second_sem)
            self.near[2].start()
            self.near[3].start()

        def third(self):
            for i, (c, d) in enumerate(zip(*self.last)):
                both = self.f_span(i)
                arrived(both, self.f_sem[i])
                c.start()
                d.start()

        def f_span(self, i):
            return self.span(1) if len(self.part) == 1 else self.two

        def own_ready(self):
            arrived(self.span(1), self.own_sem)

        def near_ready(self):
            arrived(self.span(2), self.near_sem)

        def far_ready(self):
            arrived(self.span(1), self.far_sem)

    class Gather4:
        def __init__(self, at, own, span, snd, share=None):
            lft, rgt = wrap(col - 1, ny), wrap(col + 1, ny)
            self.span = span
            first = new("recv")
            self.first_sem = first
            self.second_sem, self.third_sem = (new("recv"), new("recv")) if share is None else (share, share)
            self.a0 = remote(own(0), at(col, 0), y_plus, snd, first)
            self.b1 = remote(own(1), at(col, 1), y_minus, snd, first)
            self.a1 = remote(own(1), at(col, 1), y_plus, snd, self.second_sem)
            self.b0 = remote(own(0), at(col, 0), y_minus, snd, self.second_sem)
            self.f0 = remote(at(lft, 0), at(lft, 0), y_plus, snd, self.third_sem)
            self.f1 = remote(at(rgt, 1), at(rgt, 1), y_minus, snd, self.third_sem)

        def start(self):
            for c in (self.a0, self.b1, self.a1, self.b0):
                c.start()

        def forward(self):
            arrived(self.span(1), self.first_sem)
            self.f0.start()
            self.f1.start()

        def second(self):
            arrived(self.span(1), self.second_sem)

        def third(self):
            arrived(self.span(1), self.third_sem)

        def rest(self):
            arrived(self.span(2), self.second_sem)

    def peers():
        for dx in (1, nx - 1, 2, 0):
            for dc in (0, 1):
                if dx == 0 and dc == 0:
                    continue
                px = wrap(x + dx, nx)
                pc = core if dc == 0 else 1 - core
                yield 2 * px + pc, px, pc

    hk, qk = kb // 2, kb // 4
    sem_qr, sem_g, sem_mid, sem_r = [new("local"), new("local")], new("local"), new("local"), new("local")
    for i, (h, j) in enumerate(((0, 0), (1, 0), (0, 1), (1, 1))):
        local(qr_ref.at[pl.ds(h * hk + j * qk, qk)], qr_f.at[h, pl.ds(j * qk, qk)], sem_qr[i // 2])

    barrier = pltpu.get_barrier_semaphore()
    others = [r for r, _, _ in peers()]
    for r in others:
        pl.semaphore_signal(barrier, inc=1, device_id={"row": r}, device_id_type=MESH)
    for d in (y_plus, y_minus):
        pl.semaphore_signal(barrier, inc=1, device_id=d, device_id_type=MESH)

    load_ql = local(ql_ref, ql_f)
    for h in (0, 1):
        local(g_ref.at[:, pl.ds(h * kb, kb)], grow.at[2 * col + h], sem_g)

    def loaded(ref, sem):
        pltpu.make_async_remote_copy(
            src_ref=ref, dst_ref=ref, send_sem=send_sem.at[0], recv_sem=local_sem.at[sem],
            device_id=partner, device_id_type=MESH).wait_recv()

    def round_qr(j):
        loaded(qr_f.at[0], sem_qr[j])
        for h in (0, 1):
            qr_b[row, h, pl.ds(j * qk, qk)] = qr_f[h, pl.ds(j * qk, qk)].astype(BF16)

    round_qr(0)
    pl.semaphore_wait(barrier, len(others) + 2)

    gather_qr = Gather8(lambda s, h: qr_b.at[s, h], lambda h: qr_b.at[row, h], lambda n: qr_b.at[pl.ds(0, n)], snd_qr,
                        lambda ref: [ref.at[pl.ds(j * kb // 8, kb // 8)] for j in range(4)],
                        lambda ref: [ref.at[pl.ds(j * qk, qk)] for j in (0, 1)])
    gather_qr.a0[0].start()
    gather_qr.b1[0].start()
    round_qr(1)
    gather_qr.a0[1].start()
    gather_qr.b1[1].start()
    gather_qr.later()
    gather_qr.to_partner()
    gather_ql = Gather4(lambda s, h: ql_row.at[s, h], lambda h: ql_row.at[col, h], lambda n: ql_row.at[pl.ds(0, n)], snd_small, new("recv"))
    load_ql.wait()
    ql_row[col] = ql_f[...].astype(BF16).reshape(2, hr, lb)
    gather_ql.start()
    loaded(grow.at[pl.ds(0, 2)], sem_g)
    gather_g = Gather4(lambda s, h: grow.at[2 * s + h], lambda h: grow.at[2 * col + h],
                       lambda n: grow.at[pl.ds(0, 2 * n)], snd_g)
    gather_g.start()

    local(m_ref, mbuf, sem_mid)
    local(v_ref, vbuf, sem_mid)
    local(w_ref, wbuf, sem_mid)
    for h in (0, 1):
        local(g_ref.at[:, pl.ds(h * kb, kb)], gy.at[row, h], sem_mid)
        local(r_ref.at[:, pl.ds(h * kb, kb)], or_ref.at[h], sem_r)
    load_l = local(l_ref, ol_ref)

    def cast_block(s):
        growb[s] = grow[s].astype(BF16)

    for h in (0, 1):
        cast_block(2 * col + h)

    lft_c, rgt_c, far_c = wrap(col - 1, ny), wrap(col + 1, ny), wrap(col + 2, ny)
    x_lft, x_rgt, x_far = wrap(x - 1, nx), wrap(x + 1, nx), wrap(x + 2, nx)
    half_l = lb // 2
    quarter = pl.ds(pl.multiple_of(col * qb, qb), qb)
    row_far = wrap(row + 4, nrow)
    prow_far = row_far + 1 - 2 * core
    gather_ql.forward()
    gather_g.forward()
    gather_qr.forward()
    gather_ql.rest()

    for k in range(ny):
        block = ql_row[k].reshape(rb, lb)
        for h in (0, 1):
            ql_send[2 * k + h] = block[:, h * half_l:(h + 1) * half_l]
    ql_col[row, col] = ql_send[row, quarter]
    rcv_ql = new("recv")
    for r, _, _ in peers():
        remote(ql_send.at[r, quarter], ql_col.at[row, col], {"row": r}, snd_ql, rcv_ql).start()

    cast_block(2 * lft_c)
    cast_block(2 * rgt_c + 1)
    gather_g.second()
    cast_block(2 * lft_c + 1)
    cast_block(2 * rgt_c)
    gather_g.third()

    eb = qb // 2
    gx[row, col] = grow[row, quarter]
    rcv_gx, rest_gx = [new("recv") for _ in (0, 1)], new("recv")

    def send_gx(w):
        here = pl.ds(pl.multiple_of(col * qb + w * eb, eb), eb)
        for r, _, _ in peers():
            remote(grow.at[r, here], gx.at[row, col, pl.ds(w * eb, eb)], {"row": r}, snd_gx, rcv_gx[w]).start()

    def gather_wave(w):
        there, half = pl.ds(w * eb, eb), nrow // 2
        arrived(gx.at[pl.ds(0, nrow - 1), 0, pl.ds(0, eb)], rcv_gx[w])
        g = Gather4(lambda s, h: gx.at[pl.ds(h * half, half), s, there],
                    lambda h: gx.at[pl.ds(h * half, half), col, there],
                    lambda n: gx.at[:, pl.ds(0, n), there], snd_g, rest_gx)
        g.start()
        return g

    send_gx(0)

    def rows_of(w):
        return pl.ds(0, rb // 4) if w == 0 else pl.ds(rb // 4, rb - rb // 4)

    share_y = [new("recv") for _ in range(3)]

    gather_y = [Gather8(lambda s, h, w=w: gy.at[s, h, rows_of(w)], lambda h, w=w: grow.at[2 * col + h, rows_of(w)],
                        lambda n, w=w: gy.at[pl.ds(0, n), :, rows_of(w)], snd_rows, share=share_y) for w in (0, 1)]
    for g in gather_y:
        g.to_partner()
    cast_block(2 * far_c)
    cast_block(2 * far_c + 1)

    def turn(k):
        for j in range(4):
            qr_t[k, j] = qr_b[2 * k + j // 2, j % 2].T

    def h_part(r):
        return dot(growb[r], qr_b[r].reshape(kb, cb), NN)

    gather_qr.own_ready()
    acc[...] = h_part(2 * x) + h_part(2 * x + 1)
    gather_qr.second()
    gather_qr.near_ready()
    acc[...] += h_part(2 * x_lft) + h_part(2 * x_lft + 1)
    acc[...] += h_part(2 * x_rgt) + h_part(2 * x_rgt + 1)
    turn(x)
    turn(x_lft)
    turn(x_rgt)
    gather_qr.third()
    acc[...] += h_part(row_far)
    gather_qr.far_ready()
    hb[row] = (acc[...] + h_part(prow_far)).astype(BF16).reshape(2, hr, cb)

    def halves(ref):
        return [ref.at[pl.ds(j * hr // 2, hr // 2)] for j in (0, 1)]

    gather_h = Gather8(lambda s, h: hb.at[s, h], lambda h: hb.at[row, h], lambda n: hb.at[pl.ds(0, n)], snd_rows, halves)
    gather_h.start()

    arrived(ql_col.at[pl.ds(0, nrow - 1), 0], rcv_ql)
    gather_qc = Gather4(
        lambda s, h: ql_col.at[pl.ds(h * (nrow // 2), nrow // 2), s],
        lambda h: ql_col.at[pl.ds(h * (nrow // 2), nrow // 2), col],
        lambda n: ql_col.at[:, pl.ds(0, n)], snd_small, new("recv"))
    gather_qc.start()
    gather_qc.forward()
    gather_gx0 = gather_wave(0)

    def g_part(r):
        return dot(ql_col[r].reshape(rb, rb), hb[r].reshape(rb, cb), TN)

    def g_pair(cx):
        left = ql_col[pl.ds(2 * cx, 2)].reshape(2 * rb, rb)
        return dot(left, hb[pl.ds(2 * cx, 2)].reshape(2 * rb, cb), TN)

    gather_h.forward()
    send_gx(1)
    gather_y[0].early()
    turn(x_far)
    gather_qc.rest()
    gather_h.own_ready()
    gacc[...] = g_pair(x)
    gather_h.second()
    gather_gx0.forward()
    gather_h.near_ready()
    gacc[...] += g_pair(x_lft)
    gacc[...] += g_pair(x_rgt)
    gather_h.third()
    gacc[...] += g_part(row_far)
    gather_h.far_ready()
    rotated = gacc[...] + g_part(prow_far)

    loaded(gy.at[pl.ds(0, 4)], sem_mid)
    gacc[...] = rotated
    gather_n = Gather8(lambda s, h: nb.at[s, h], lambda h: nb.at[row, h], lambda n: nb.at[pl.ds(0, n)], snd_rows,
                       halves, halves)
    for j in (0, 1):
        for h in (0, 1):
            part = pl.ds(h * hr + j * (hr // 2), hr // 2)
            turned = gacc[part]
            new_first = BETA1 * mbuf[part] + (1.0 - BETA1) * turned
            new_second = BETA2 * vbuf[part] + (1.0 - BETA2) * turned * turned
            below = BIAS_ONE * jnp.sqrt(new_second * (1.0 / BIAS_TWO)) + BIAS_ONE * EPS
            nb[row, h, pl.ds(j * (hr // 2), hr // 2)] = (new_first / below).astype(BF16)
            om_ref[part] = new_first
            ov_ref[part] = new_second
        gather_n.a0[j].start()
        gather_n.b1[j].start()
    gather_n.later()
    gather_n.to_partner()
    gather_gx1 = gather_wave(1)

    def k_part(r):
        return dot(ql_send[r], nb[r].reshape(rb, cb), NN)

    def k_pair(cx):
        return dot(ql_row[cx].reshape(rb, lb), nb[pl.ds(2 * cx, 2)].reshape(2 * rb, cb), NN)

    gather_n.own_ready()
    acc[...] = k_pair(x)
    gather_n.forward()
    gather_y[0].later()
    gather_y[1].early()
    gather_y[1].later()
    gather_gx1.forward()
    gather_n.second()
    gather_n.near_ready()
    acc[...] += k_pair(x_lft)
    acc[...] += k_pair(x_rgt)
    gather_n.third()
    acc[...] += k_part(row_far)
    gather_n.far_ready()
    back = (acc[...] + k_part(prow_far)).astype(BF16)

    rcv_u, rcv_f = new("recv"), [new("recv"), new("recv")]

    def half(k, h):
        return up.at[k, pl.ds(2 * h, 2)]

    u_far = [remote(half(far_c, 0), rin.at[0], y_plus, snd_u, rcv_f[0]),
             remote(half(far_c, 1), rin.at[1], y_minus, snd_u, rcv_f[1])]
    u_half = [remote(half(rgt_c, 1), rin.at[2], y_plus, snd_u, rcv_u),
              remote(half(lft_c, 0), rin.at[3], y_minus, snd_u, rcv_u)]
    u_sum = [remote(half(rgt_c, 0), rin.at[4], y_plus, snd_u, rcv_u),
             remote(half(lft_c, 1), rin.at[5], y_minus, snd_u, rcv_u)]

    def make_u(k):
        for j in range(4):
            up[k, j] = dot(back, qr_t[k, j], NN)

    make_u(far_c)
    for c in u_far:
        c.start()
    make_u(rgt_c)
    u_half[0].start()
    make_u(lft_c)
    u_half[1].start()
    gather_y[0].forward()
    make_u(col)

    arrived(gx.at[:, pl.ds(0, 2)], rest_gx)
    right_g = gx[pl.ds(2 * col, 2)].reshape(2 * rb, kb)
    lp[...] = dot(gx[...].reshape(nrow * rb, kb), right_g, NT, HIGHEST).reshape(nrow, rb, lb)
    rcv_s = new("recv")
    for k in range(nx):
        remote(lp.at[2 * k + 1 - core], lrecv.at[k], partner, snd_small, rcv_s).start()

    def add_r(cx, first=False):
        left = gx[pl.ds(2 * cx, 2)].reshape(2 * rb, kb)

        def body(h, _):
            part = dot(left, gy[pl.ds(2 * cx, 2), h].reshape(2 * rb, kb), TN, HIGHEST)
            old = or_ref[h]
            if first:
                old = BETA2 * old
            or_ref[h] = old + (1.0 - BETA2) * part
            return 0

        lax.fori_loop(0, 2, body, 0)

    gather_y[0].second()
    gather_y[1].forward()
    loaded(or_ref, sem_r)
    arrived(gy.at[pl.ds(0, 1)], share_y[0])
    add_r(x, True)

    arrived(rin.at[0], rcv_f[0])
    up[rgt_c, :2] = up[rgt_c, :2] + rin[0]
    u_sum[0].start()
    arrived(rin.at[1], rcv_f[1])
    up[lft_c, 2:] = up[lft_c, 2:] + rin[1]
    u_sum[1].start()

    arrived(lrecv, rcv_s)
    for k in range(nx):
        lp[2 * k + core] = lp[2 * k + core] + lrecv[k]
    rcv_l = new("recv")
    for dx in (1, nx - 1, 2):
        to = 2 * wrap(x + dx, nx) + core
        remote(lp.at[to], lx.at[x], {"row": to}, snd_small, rcv_l).start()

    gather_y[1].second()
    arrived(gy.at[pl.ds(0, 2)], share_y[1])
    add_r(x_lft)
    gather_y[0].third()
    add_r(x_rgt)
    gather_y[1].third()
    arrived(gy.at[pl.ds(0, 1)], share_y[2])
    add_r(x_far)

    load_l.wait()
    arrived(lx.at[pl.ds(0, nx - 1)], rcv_l)
    total = lp[row]
    for dx in (1, 2, 3):
        total = total + lx[wrap(x + dx, nx)]
    ol_ref[...] = BETA2 * ol_ref[...] + (1.0 - BETA2) * total

    arrived(rin.at[pl.ds(0, 4)], rcv_u)
    for j in range(4):
        cols = pl.ds(j * (cb // 4), cb // 4)
        others_sum = (rin[3, j] + rin[4, j]) if j < 2 else (rin[2, j - 2] + rin[5, j - 2])
        ow_ref[:, cols] = wbuf[:, cols] - LR * (up[col, j] + others_sum)

    assert tuple(counts.values()) == COUNTS
    for c in pending:
        c.wait_send()


def write_out(w_ref, m_ref, v_ref, l_ref, r_ref, ow_ref, om_ref, ov_ref, ol_ref, or_ref, sem):
    kb = r_ref.shape[1]
    moves = [(w_ref, ow_ref), (m_ref, om_ref), (v_ref, ov_ref), (l_ref, ol_ref)]
    moves += [(r_ref.at[h], or_ref.at[:, pl.ds(h * kb, kb)]) for h in (0, 1)]
    copies = [pltpu.make_async_copy(a, b, sem.at[i]) for i, (a, b) in enumerate(moves)]
    for c in copies:
        c.start()
    for c in copies:
        c.wait()


def solution(mesh):
    nx, ny = mesh.shape["row"] // 2, mesh.shape["col"]
    tile_spec = P(("layer", "row"), "col")

    def local_step(*args):
        rb, cb = args[0].shape
        kb = args[7].shape[0]
        lb = args[6].shape[1]
        hr, nr = rb // 2, 2 * nx
        vm = pltpu.VMEM
        shapes = [args[0], args[2], args[3], args[4], args[5]]
        held = pl.pallas_call(
            functools.partial(kernel, nx, ny),
            out_shape=tuple(vm(s, F32) for s in [(rb, cb)] * 3 + [(rb, lb), (2, kb, kb)]),
            in_specs=[pl.BlockSpec(memory_space=pl.ANY)] * 8,
            out_specs=tuple([pl.BlockSpec(memory_space=pltpu.VMEM)] * 5),
            scratch_shapes=[
                vm((2, kb // 2, cb), F32),
                vm((nr, 2, kb // 2, cb), BF16),
                vm((nx, 4, cb, kb // 2), BF16),
                vm((nr, rb, kb), F32),
                vm((nr, rb, kb), BF16),
                vm((rb, lb), F32),
                vm((ny, 2, hr, lb), BF16),
                vm((nr, rb, lb // 2), BF16),
                vm((nr, ny, rb // ny, lb // 2), BF16),
                vm((nr, ny, rb // ny, kb), F32),
                vm((nr, 2, rb, kb), F32),
                vm((nr, 2, hr, cb), BF16),
                vm((nr, 2, hr, cb), BF16),
                vm((rb, cb), F32),
                vm((rb, cb), F32),
                vm((ny, 4, rb, cb // 4), F32),
                vm((6, 2, rb, cb // 4), F32),
                vm((nr, rb, lb), F32),
                vm((nx, rb, lb), F32),
                vm((nx, rb, lb), F32),
                vm((rb, cb), F32),
                vm((rb, cb), F32),
                vm((rb, cb), F32),
                *[pltpu.SemaphoreType.DMA((n,)) for n in COUNTS],
            ],
            compiler_params=pltpu.CompilerParams(
                collective_id=0, has_side_effects=True, vmem_limit_bytes=61600 * 1024),
        )(*args)
        return pl.pallas_call(
            write_out,
            out_shape=tuple(jax.ShapeDtypeStruct(s.shape, s.dtype) for s in shapes),
            in_specs=[pl.BlockSpec(memory_space=pltpu.VMEM)] * 5,
            out_specs=tuple([pl.BlockSpec(memory_space=pl.ANY)] * 5),
            scratch_shapes=[pltpu.SemaphoreType.DMA((6,))],
            compiler_params=pltpu.CompilerParams(vmem_limit_bytes=4 * 1024 * 1024),
        )(*held)

    return jax.shard_map(local_step, mesh=mesh, in_specs=(tile_spec,) * 8, out_specs=(tile_spec,) * 5, check_vma=False)
```

profile of v0, /device:TPU:97, one launch (start us, length us, event | category | flops | bytes accessed | tf_op | source)
XLA Modules:
  0.0 94.0 jit_solution(733845202375531220)
XLA Ops:
  0.6 91.2 %shard_map.119 = (f32[128,1024]{1,0:T(8,128)S(1)}, f32[128,1024]{1,0:T(8,128)S(1)}, f32[128,1024]{1,0:T(8,128)S(1)}, f32[128,256]{1,0:T(8,128)S(1)}, f32[2,512,512]{2,1,0:T(8,128)S(1)}) custom-call(f32[128,1024]{1,0:T(8,128)} %w_ref.1, f32[128,1024]{1,0:T(8,128)} %g_ref.1, f32[128,1024]{1,0:T(8,128)} %m_ref.1, f32[128,1024]{1,0:T(8,128)} %v_ref.1, ...), custom_call_target="tpu_custom_call" | custom-call | tf_op jit(solution)/shard_map/pallas_call | solution.py:540
  91.9 1.9 %shard_map.120 = (f32[128,1024]{1,0:T(8,128)}, f32[128,1024]{1,0:T(8,128)}, f32[128,1024]{1,0:T(8,128)}, f32[128,256]{1,0:T(8,128)}, f32[512,1024]{1,0:T(8,128)}) custom-call(f32[128,1024]{1,0:T(8,128)S(1)} %get-tuple-element.10.w_ref, f32[128,1024]{1,0:T(8,128)S(1)} %get-tuple-element.11.m_ref, f32[128,1024]{1,0:T(8,128)S(1)} %get-tuple-element.12.v_ref, ...), custom_call_target="tpu_custom_call" | custom-call | tf_op jit(solution)/shard_map/pallas_call | solution.py:574
where the time goes:
time: 94.1 us; the launch traced here: 94 us
  Pallas kernels  93.2 us (99%)
    pallas_call x1, Pallas kernels, local_step(): pl.pallas_call(functools.partial(kernel, nx, ny), out_shape=tuple((vm(s,...  91.2 us
    pallas_call x1, Pallas kernels, local_step(): pl.pallas_call(write_out, out_shape=tuple((jax.ShapeDtypeStruct(s.shape,...  1.93 us

commit v1 on v0

--- a/solution.py
+++ b/solution.py
@@ -332,9 +332,6 @@
     gather_qr.near_ready()
     acc[...] += h_part(2 * x_lft) + h_part(2 * x_lft + 1)
     acc[...] += h_part(2 * x_rgt) + h_part(2 * x_rgt + 1)
-    turn(x)
-    turn(x_lft)
-    turn(x_rgt)
     gather_qr.third()
     acc[...] += h_part(row_far)
     gather_qr.far_ready()
@@ -344,7 +341,11 @@
         return [ref.at[pl.ds(j * hr // 2, hr // 2)] for j in (0, 1)]
 
     gather_h = Gather8(lambda s, h: hb.at[s, h], lambda h: hb.at[row, h], lambda n: hb.at[pl.ds(0, n)], snd_rows, halves)
-    gather_h.start()
+    gather_h.early()
+    gather_h.to_partner()
+    turn(x_lft)
+    turn(x_rgt)
+    gather_h.later()
 
     arrived(ql_col.at[pl.ds(0, nrow - 1), 0], rcv_ql)
     gather_qc = Gather4(
@@ -365,7 +366,6 @@
     gather_h.forward()
     send_gx(1)
     gather_y[0].early()
-    turn(x_far)
     gather_qc.rest()
     gather_h.own_ready()
     gacc[...] = g_pair(x)
@@ -395,8 +395,10 @@
             ov_ref[part] = new_second
         gather_n.a0[j].start()
         gather_n.b1[j].start()
+    gather_n.to_partner()
+    turn(x)
+    turn(x_far)
     gather_n.later()
-    gather_n.to_partner()
     gather_gx1 = gather_wave(1)
 
     def k_part(r):
@@ -517,8 +519,10 @@
 
 def write_out(w_ref, m_ref, v_ref, l_ref, r_ref, ow_ref, om_ref, ov_ref, ol_ref, or_ref, sem):
     kb = r_ref.shape[1]
-    moves = [(w_ref, ow_ref), (m_ref, om_ref), (v_ref, ov_ref), (l_ref, ol_ref)]
-    moves += [(r_ref.at[h], or_ref.at[:, pl.ds(h * kb, kb)]) for h in (0, 1)]
+    part = kb // 4
+    moves = [(r_ref.at[h, pl.ds(j * part, part)], or_ref.at[pl.ds(j * part, part), pl.ds(h * kb, kb)])
+             for j in range(4) for h in (0, 1)]
+    moves += [(w_ref, ow_ref), (m_ref, om_ref), (v_ref, ov_ref), (l_ref, ol_ref)]
     copies = [pltpu.make_async_copy(a, b, sem.at[i]) for i, (a, b) in enumerate(moves)]
     for c in copies:
         c.start()
@@ -576,7 +580,7 @@
             out_shape=tuple(jax.ShapeDtypeStruct(s.shape, s.dtype) for s in shapes),
             in_specs=[pl.BlockSpec(memory_space=pltpu.VMEM)] * 5,
             out_specs=tuple([pl.BlockSpec(memory_space=pl.ANY)] * 5),
-            scratch_shapes=[pltpu.SemaphoreType.DMA((6,))],
+            scratch_shapes=[pltpu.SemaphoreType.DMA((12,))],
             compiler_params=pltpu.CompilerParams(vmem_limit_bytes=4 * 1024 * 1024),
         )(*held)
 

time: 94.1 us -> 94.2 us (level)
  no operation moved by 1% of the time
where the time goes in v1:
time: 94.2 us; the launch traced here: 94.1 us
  Pallas kernels  93.3 us (99%)
    pallas_call x1, Pallas kernels, local_step(): pl.pallas_call(functools.partial(kernel, nx, ny), out_shape=tuple((vm(s,...  91.3 us
    pallas_call x1, Pallas kernels, local_step(): pl.pallas_call(write_out, out_shape=tuple((jax.ShapeDtypeStruct(s.shape,...  1.97 us

profile of v1, /device:TPU:97, one launch (start us, length us, event | category | flops | bytes accessed | tf_op | source)
XLA Modules:
  0.0 94.1 jit_solution(13252524658275995647)
XLA Ops:
  0.6 91.3 %shard_map.119 = (f32[128,1024]{1,0:T(8,128)S(1)}, f32[128,1024]{1,0:T(8,128)S(1)}, f32[128,1024]{1,0:T(8,128)S(1)}, f32[128,256]{1,0:T(8,128)S(1)}, f32[2,512,512]{2,1,0:T(8,128)S(1)}) custom-call(f32[128,1024]{1,0:T(8,128)} %w_ref.1, f32[128,1024]{1,0:T(8,128)} %g_ref.1, f32[128,1024]{1,0:T(8,128)} %m_ref.1, f32[128,1024]{1,0:T(8,128)} %v_ref.1, ...), custom_call_target="tpu_custom_call" | custom-call | tf_op jit(solution)/shard_map/pallas_call | solution.py:544
  91.9 2.0 %shard_map.120 = (f32[128,1024]{1,0:T(8,128)}, f32[128,1024]{1,0:T(8,128)}, f32[128,1024]{1,0:T(8,128)}, f32[128,256]{1,0:T(8,128)}, f32[512,1024]{1,0:T(8,128)}) custom-call(f32[128,1024]{1,0:T(8,128)S(1)} %get-tuple-element.10.w_ref, f32[128,1024]{1,0:T(8,128)S(1)} %get-tuple-element.11.m_ref, f32[128,1024]{1,0:T(8,128)S(1)} %get-tuple-element.12.v_ref, ...), custom_call_target="tpu_custom_call" | custom-call | tf_op jit(solution)/shard_map/pallas_call | solution.py:578

commit v2 on v0

--- a/solution.py
+++ b/solution.py
@@ -308,7 +308,7 @@
     send_gx(0)
 
     def rows_of(w):
-        return pl.ds(0, rb // 4) if w == 0 else pl.ds(rb // 4, rb - rb // 4)
+        return pl.ds(w * hr, hr)
 
     share_y = [new("recv") for _ in range(3)]
 

time: 94.1 us -> 93.5 us (level)
  no operation moved by 1% of the time
where the time goes in v2:
time: 93.5 us; the launch traced here: 93.4 us
  Pallas kernels  92.6 us (99%)
    pallas_call x1, Pallas kernels, local_step(): pl.pallas_call(functools.partial(kernel, nx, ny), out_shape=tuple((vm(s,...  90.6 us
    pallas_call x1, Pallas kernels, local_step(): pl.pallas_call(write_out, out_shape=tuple((jax.ShapeDtypeStruct(s.shape,...  1.93 us

profile of v2, /device:TPU:97, one launch (start us, length us, event | category | flops | bytes accessed | tf_op | source)
XLA Modules:
  0.0 93.4 jit_solution(1290677773240606771)
XLA Ops:
  0.6 90.6 %shard_map.119 = (f32[128,1024]{1,0:T(8,128)S(1)}, f32[128,1024]{1,0:T(8,128)S(1)}, f32[128,1024]{1,0:T(8,128)S(1)}, f32[128,256]{1,0:T(8,128)S(1)}, f32[2,512,512]{2,1,0:T(8,128)S(1)}) custom-call(f32[128,1024]{1,0:T(8,128)} %w_ref.1, f32[128,1024]{1,0:T(8,128)} %g_ref.1, f32[128,1024]{1,0:T(8,128)} %m_ref.1, f32[128,1024]{1,0:T(8,128)} %v_ref.1, ...), custom_call_target="tpu_custom_call" | custom-call | tf_op jit(solution)/shard_map/pallas_call | solution.py:540
  91.3 1.9 %shard_map.120 = (f32[128,1024]{1,0:T(8,128)}, f32[128,1024]{1,0:T(8,128)}, f32[128,1024]{1,0:T(8,128)}, f32[128,256]{1,0:T(8,128)}, f32[512,1024]{1,0:T(8,128)}) custom-call(f32[128,1024]{1,0:T(8,128)S(1)} %get-tuple-element.10.w_ref, f32[128,1024]{1,0:T(8,128)S(1)} %get-tuple-element.11.m_ref, f32[128,1024]{1,0:T(8,128)S(1)} %get-tuple-element.12.v_ref, ...), custom_call_target="tpu_custom_call" | custom-call | tf_op jit(solution)/shard_map/pallas_call | solution.py:574
